TPU v7x, 64 devices: a 2x2x8 block of a 4x4x8 slice. The times are simulated.
64 devices in a mesh: rep: 4 (over x, y), dp: 16 (over z, core).
Axes of the slice: x: 2, y: 2, z: 8, core: 2. Of those that a mesh axis runs over, the one named last changes fastest.
The devices are a block of a 4x4x8 slice.
Arguments:
- g_w_gate: bfloat16 [64, 2, 640, 2176], P(('rep', 'dp')), parts along dimension 0
- g_w_up: bfloat16 [64, 2, 640, 2176], P(('rep', 'dp')), parts along dimension 0
- g_w_down: bfloat16 [64, 2, 2176, 640], P(('rep', 'dp')), parts along dimension 0
- w_gate: bfloat16 [2, 640, 2176], replicated
- w_up: bfloat16 [2, 640, 2176], replicated
- w_down: bfloat16 [2, 2176, 640], replicated
- m_w_gate: float32 [2, 640, 2176], P(None, 'dp')
- m_w_up: float32 [2, 640, 2176], P(None, 'dp')
- m_w_down: float32 [2, 2176, 640], P(None, 'dp')
- v_w_gate: float32 [2, 640, 2176], P(None, 'dp')
- v_w_up: float32 [2, 640, 2176], P(None, 'dp')
- v_w_down: float32 [2, 2176, 640], P(None, 'dp')
Outputs:
- output 1: bfloat16 [8, 640, 2176], P('rep'), parts along dimension 0
- output 2: bfloat16 [8, 640, 2176], P('rep'), parts along dimension 0
- output 3: bfloat16 [8, 2176, 640], P('rep'), parts along dimension 0
- output 4: float32 [8, 640, 2176], P('rep', 'dp'), parts along dimension 0
- output 5: float32 [8, 640, 2176], P('rep', 'dp'), parts along dimension 0
- output 6: float32 [8, 2176, 640], P('rep', 'dp'), parts along dimension 0
- output 7: float32 [8, 640, 2176], P('rep', 'dp'), parts along dimension 0
- output 8: float32 [8, 640, 2176], P('rep', 'dp'), parts along dimension 0
- output 9: float32 [8, 2176, 640], P('rep', 'dp'), parts along dimension 0
There are 4 independent parts. A program takes and returns all parts, laid end to end along the dimension named above; an argument that names none is the same for every part.
All inputs are finite; a program needn't handle non-finite values.
Results may differ from a plain program's by a relative error of at most 0.022.
Values are sent between devices in bfloat16 or wider.
A program may use at most 768 MiB of HBM per device.

v0:
```python
import jax
import jax.numpy as jnp
from jax import lax
from jax.sharding import PartitionSpec as P


def adamw(w, m, v, g):
    m = 0.9 * m + 0.1 * g
    v = 0.95 * v + 0.05 * g * g
    step = m * lax.rsqrt(v + 1e-8) + 0.1 * w
    return (w - 0.02 * step).astype(jnp.bfloat16), m, v


def clipped(gradients, sum_of_squares, count):
    factor = jnp.minimum(1.0, 0.5 * lax.rsqrt(sum_of_squares / count + 1e-30))
    return [g * factor for g in gradients]


def solution(mesh):
    def step(*arrays):
        terms, weights, m, v = (arrays[i : i + 3] for i in (0, 3, 6, 9))
        gradients = [lax.psum_scatter(t[0], "dp", scatter_dimension=1, tiled=True).astype(jnp.float32) for t in terms]
        squares = lax.psum(sum(jnp.sum(g * g) for g in gradients), "dp")
        gradients = clipped(gradients, squares, lax.psum(1, "dp") * sum(g.size for g in gradients))
        me = lax.axis_index("dp")
        own = [lax.dynamic_slice_in_dim(w, me * one.shape[1], one.shape[1], 1).astype(jnp.float32) for w, one in zip(weights, m, strict=True)]
        new = [adamw(w, m, v, g) for w, m, v, g in zip(own, m, v, gradients, strict=True)]
        whole = [lax.all_gather(one[0], "dp", axis=1, tiled=True) for one in new]
        return (*whole, *(one[1] for one in new), *(one[2] for one in new))

    all_of, cut = P(None, None, None), P(None, "dp", None)
    return jax.shard_map(
        step,
        mesh=mesh,
        in_specs=(P(("rep", "dp"), None, None, None),) * 3 + (all_of,) * 3 + (cut,) * 6,
        out_specs=(P("rep", None, None),) * 3 + (P("rep", "dp", None),) * 6,
        check_vma=False,
    )
```

profile of v0, /device:TPU:21, one launch (start us, length us, event | category | flops | bytes accessed | tf_op | source)
XLA Modules:
  0.0 391.9 jit_solution(17164134420730224620)
XLA Ops:
  7.2 0.1 reduce-scatter.10.cloned.1.call-start
  7.3 9.9 %copy.21 = bf16[2,640,2176]{2,0,1:T(2,128)(2,1)S(1)} copy(bf16[2,640,2176]{2,1,0:T(8,128)(2,1)} %bitcast.21) | data formatting | bytes 11141120
  17.2 3.3 copy.27
  20.6 0.1 reduce-scatter.10.cloned.1.call-update
  20.6 0.1 reduce-scatter.14.cloned.1.call-start
  20.7 25.9 %copy.25 = bf16[2,2176,640]{2,0,1:T(2,128)(2,1)S(1)} copy(bf16[2,2176,640]{2,1,0:T(8,128)(2,1)} %bitcast.22) | data formatting | bytes 11141120
  46.6 3.4 copy.29
  50.0 0.1 reduce-scatter.14.cloned.1.call-update
  50.1 0.1 reduce-scatter.12.cloned.1.call-start
  50.2 9.9 %copy.23 = bf16[2,640,2176]{2,0,1:T(2,128)(2,1)S(1)} copy(bf16[2,640,2176]{2,1,0:T(8,128)(2,1)} %bitcast.23) | data formatting | bytes 11141120
  60.1 3.3 copy.28
  63.5 0.0 copy-start.2
  63.5 0.0 copy-start.3
  63.5 0.0 copy-start.4
  63.5 0.1 reduce-scatter.12.cloned.1.call-update
  63.5 0.1 all-gather.8.cloned.1.call-start
  63.6 21.3 %reduce-scatter.10.cloned.1.call-done = bf16[40,4352]{1,0:T(8,128)(2,1)} async-done(((bf16[640,4352]{1,0:T(8,128)(2,1)}), bf16[40,4352]{1,0:T(8,128)(2,1)}) %reduce-scatter.10.cloned.1.call-update) | async-done | bytes 348176
  84.9 1.1 reshape.19
  86.0 63.1 %reduce-scatter.14.cloned.1.call-done = bf16[136,1280]{1,0:T(8,128)(2,1)} async-done(((bf16[2176,1280]{1,0:T(8,128)(2,1)}), bf16[136,1280]{1,0:T(8,128)(2,1)}) %reduce-scatter.14.cloned.1.call-update) | async-done | bytes 348176
  149.1 1.1 reshape.23
  150.2 0.8 fusion.11
  151.0 62.4 %reduce-scatter.12.cloned.1.call-done = bf16[40,4352]{1,0:T(8,128)(2,1)} async-done(((bf16[640,4352]{1,0:T(8,128)(2,1)}), bf16[40,4352]{1,0:T(8,128)(2,1)}) %reduce-scatter.12.cloned.1.call-update) | async-done | bytes 348176
  213.3 1.1 reshape.21
  214.4 0.8 fusion.9
  217.1 27.3 %psum.7 = f32[]{:T(128)} all-reduce(f32[]{:T(128)S(6)} %add.65), channel_id=1, replica_groups=mesh['rep'=4,'dp'=16] {'dp'}, use_global_device_ids=true, to_apply=%region_6.0 | all-reduce | flops 1 | bytes 8 | tf_op jit(solution)/shard_map/psum | solution.py:23
  245.2 0.0 copy-done.2
  245.2 0.0 copy-done.3
  245.2 2.4 fusion.17
  247.6 0.1 all-gather.8.cloned.1.call-update
  247.6 0.1 all-gather.4.cloned.1.call-start
  247.7 0.0 copy-done.4
  247.7 2.6 fusion.8
  250.3 0.1 all-gather.4.cloned.1.call-update
  250.4 0.1 all-gather.6.cloned.1.call-start
  250.4 2.8 fusion.14
  253.2 0.1 all-gather.6.cloned.1.call-update
  253.3 36.7 %all-gather.8.cloned.1.call-done = bf16[2,2176,640]{2,1,0:T(8,128)(2,1)} async-done(((bf16[2,136,640]{2,1,0:T(8,128)(2,1)}), bf16[2,2176,640]{2,1,0:T(8,128)(2,1)}) %all-gather.8.cloned.1.call-update) | async-done | bytes 5570576 | tf_op jit(solution)/shard_map/all_gather | solution.py:28
  290.0 41.2 %all-gather.4.cloned.1.call-done = bf16[2,640,2176]{2,1,0:T(8,128)(2,1)} async-done(((bf16[2,40,2176]{2,1,0:T(8,128)(2,1)}), bf16[2,640,2176]{2,1,0:T(8,128)(2,1)}) %all-gather.4.cloned.1.call-update) | async-done | bytes 5570576 | tf_op jit(solution)/shard_map/all_gather | solution.py:28
  331.2 41.2 %all-gather.6.cloned.1.call-done = bf16[2,640,2176]{2,1,0:T(8,128)(2,1)} async-done(((bf16[2,40,2176]{2,1,0:T(8,128)(2,1)}), bf16[2,640,2176]{2,1,0:T(8,128)(2,1)}) %all-gather.6.cloned.1.call-update) | async-done | bytes 5570576 | tf_op jit(solution)/shard_map/all_gather | solution.py:28
  372.4 0.0 copy-start.1
  372.4 5.6 %copy.48 = bf16[2,640,2176]{2,1,0:T(8,128)(2,1)} copy(bf16[2,640,2176]{2,1,0:T(8,128)(2,1)} %all-gather.4.cloned.1.call-done) | data formatting | bytes 11141120
  378.0 0.0 copy-done.1
  378.0 0.0 copy-start
  378.0 2.8 copy.49
  380.8 1.8 copy-done
  382.6 2.5 copy.50
Async XLA Ops:
  7.2 77.7 %reduce-scatter.10.cloned.1.call-start = ((), (), s32[]{:S(2)}) async-start(), calls=%async_computation.6 | async-start | bytes 5918720
  20.6 128.5 %reduce-scatter.14.cloned.1.call-start = ((), (), s32[]{:S(2)}) async-start(), calls=%async_computation.8 | async-start | bytes 5918720
  50.1 163.2 %reduce-scatter.12.cloned.1.call-start = ((), (), s32[]{:S(2)}) async-start(), calls=%async_computation.7 | async-start | bytes 5918720
  63.5 181.7 %copy-start.2 = (f32[2,136,640]{2,1,0:T(8,128)S(1)}, f32[2,136,640]{2,1,0:T(8,128)}, u32[]{:S(2)}) copy-start(f32[2,136,640]{2,1,0:T(8,128)} %param.23) | copy-start | bytes 2088964
  63.5 181.7 %copy-start.3 = (f32[2,136,640]{2,1,0:T(8,128)S(1)}, f32[2,136,640]{2,1,0:T(8,128)}, u32[]{:S(2)}) copy-start(f32[2,136,640]{2,1,0:T(8,128)} %param.20) | copy-start | bytes 2088964
  63.5 184.2 %copy-start.4 = (f32[2,40,2176]{2,1,0:T(8,128)S(1)}, f32[2,40,2176]{2,1,0:T(8,128)}, u32[]{:S(2)}) copy-start(f32[2,40,2176]{2,1,0:T(8,128)} %param.21) | copy-start | bytes 2088964
  63.5 226.5 %all-gather.8.cloned.1.call-start = ((), (), s32[]{:S(2)}) async-start(), calls=%async_computation.5 | async-start | bytes 5918720 | tf_op jit(solution)/shard_map/all_gather | solution.py:28
  247.6 83.6 %all-gather.4.cloned.1.call-start = ((), (), s32[]{:S(2)}) async-start(), calls=%async_computation.3 | async-start | bytes 5918720 | tf_op jit(solution)/shard_map/all_gather | solution.py:28
  250.4 122.0 %all-gather.6.cloned.1.call-start = ((), (), s32[]{:S(2)}) async-start(), calls=%async_computation.4 | async-start | bytes 5918720 | tf_op jit(solution)/shard_map/all_gather | solution.py:28
  372.4 5.6 %copy-start.1 = (bf16[2,640,2176]{2,1,0:T(8,128)(2,1)S(1)}, bf16[2,640,2176]{2,1,0:T(8,128)(2,1)}, u32[]{:S(2)}) copy-start(bf16[2,640,2176]{2,1,0:T(8,128)(2,1)} %all-gather.6.cloned.1.call-done) | copy-start | bytes 16711684
  378.0 4.6 %copy-start = (bf16[2,2176,640]{2,1,0:T(8,128)(2,1)S(1)}, bf16[2,2176,640]{2,1,0:T(8,128)(2,1)}, u32[]{:S(2)}) copy-start(bf16[2,2176,640]{2,1,0:T(8,128)(2,1)} %all-gather.8.cloned.1.call-done) | copy-start | bytes 16711684
Sparse Core Ops, SparseCore 0:
  20.7 64.1 reduce-scatter.9
  87.9 61.2 reduce-scatter.13
  152.1 61.2 reduce-scatter.11
  247.7 42.2 all-gather.7
  292.0 39.1 all-gather.3
  333.2 39.1 all-gather.5
where the time goes:
time: 392 us
  waiting for transfers between devices  266 us (68%)
  local copies, waits for them, and re-layouts  71.8 us (18%)
  blocking collectives  27.3 us (7%)
  between operations  16.9 us (4%)
  other arithmetic  9.36 us (2%)
    unnamed x9, waiting for transfers between devices  147 us
    all_gather x3, waiting for transfers between devices, step(): whole = [lax.all_gather(one[0], 'dp', axis=1, tiled=True) for one in new]  119 us
    unnamed x22, local copies, waits for them, and re-layouts  71.8 us
    psum x1, blocking collectives, step(): squares = lax.psum(sum((jnp.sum(g * g) for g in gradients)), 'dp')  27.3 us
  transfers between devices with their start and end apart: 6, of which 6 were waited for; matrix products, arithmetic and copies ran while one was open for 13% of the time, Pallas kernels for 0%

commit v1 on v0

v1 whole, which is shorter than its diff:
```python
import functools

import jax
import jax.numpy as jnp
from jax import lax
from jax.experimental import pallas as pl
from jax.experimental.pallas import tpu as pltpu
from jax.sharding import PartitionSpec as P

CORES = 2
ROWS = 8
WEIGHTS = 3
LANES = 128


def rows_of(ref, lead, start, count):
    return ref.at[(*lead, pl.ds(pl.multiple_of(start, ROWS), count))]


def step_kernel(n, count, *refs):
    take = iter(refs)
    three = lambda: [next(take) for _ in range(WEIGHTS)]
    grads, old, m_in, v_in = three(), three(), three(), three()
    whole, m, v = three(), three(), three()
    mine, theirs, ring = three(), three(), three()
    squares, parts = next(take), next(take)
    (load_sem, swap_send, swap_recv, ring_send, ring_recv, gather_send, gather_recv, give_send, give_recv, state_sem, part_send, part_recv) = take

    chips = n // CORES
    me = lax.axis_index("dp")
    chip, core = me // CORES, lax.rem(me, CORES)
    other = chip * CORES + 1 - core
    ahead = lax.rem(chip + 1, chips) * CORES + core
    behind = lax.rem(chip + chips - 1, chips) * CORES + core
    toward = (ahead, behind)

    def to(device):
        return dict(device_id={"dp": device}, device_id_type=pl.DeviceIdType.MESH)

    def chip_at(way, back):
        return lax.rem(chip + chips - back, chips) if way == 0 else lax.rem(chip + back, chips)

    def height(k):
        return m[k].shape[1]

    pieces = [(k, way) for k in range(WEIGHTS) for way in (0, 1)]

    def load(k, way, s):
        at = (chip_at(way, s + 1) * CORES + core) * height(k)
        return pltpu.make_async_copy(rows_of(grads[k], (0, way), at, height(k)), mine[k].at[s, way], load_sem.at[k, way, s])

    def swap(k, way, s):
        at = (chip_at(way, s + 1) * CORES + 1 - core) * height(k)
        return pltpu.make_async_remote_copy(
            rows_of(grads[k], (0, way), at, height(k)), theirs[k].at[s, way], swap_send.at[k, way, s], swap_recv.at[k, way, s], **to(other)
        )

    def hop(k, way, s):
        return pltpu.make_async_remote_copy(
            mine[k].at[s, way], ring[k].at[s, way], ring_send.at[k, way, s], ring_recv.at[k, way, s], **to(toward[way])
        )

    def place(k, way, back, at_core):
        return rows_of(whole[k], (way,), (chip_at(way, back) * CORES + at_core) * height(k), height(k))

    def pass_on(k, way, s):
        block = place(k, way, s, core)
        return pltpu.make_async_remote_copy(block, block, gather_send.at[k, way, s], gather_recv.at[k, way, s], **to(toward[way]))

    def give(k, way, s):
        block = place(k, way, s, core)
        return pltpu.make_async_remote_copy(block, block, give_send.at[k, way, s], give_recv.at[k, way, s], **to(other))

    def arrived(k, way, s):
        block = place(k, way, s + 1, core)
        return pltpu.make_async_remote_copy(block, block, gather_send.at[k, way, s], gather_recv.at[k, way, s], **to(toward[way]))

    def given(k, way, s):
        block = place(k, way, s, 1 - core)
        return pltpu.make_async_remote_copy(block, block, give_send.at[k, way, s], give_recv.at[k, way, s], **to(other))

    def state(k):
        for way in (0, 1):
            yield pltpu.make_async_copy(
                rows_of(old[k], (way,), me * height(k), height(k)), place(k, way, 0, core), state_sem.at[k, way]
            )
        yield pltpu.make_async_copy(m_in[k], m[k], state_sem.at[k, 2])
        yield pltpu.make_async_copy(v_in[k], v[k], state_sem.at[k, 3])

    def part_to(d):
        peer = lax.rem(me + d, n)
        return pltpu.make_async_remote_copy(parts.at[0], parts.at[d], part_send.at[d], part_recv.at[d], **to(peer))

    for k, way in pieces:
        load(k, way, 0).start()

    barrier = pltpu.get_barrier_semaphore()
    for device in (other, ahead, behind):
        pl.semaphore_signal(barrier, inc=1, **to(device))
    pl.semaphore_wait(barrier, 3)

    for k, way in pieces:
        swap(k, way, 0).start()

    @pl.loop(1, chips)
    def _(s):
        for k, way in pieces:
            swap(k, way, s).start()
            load(k, way, s).start()

    for k in range(WEIGHTS):
        for copy in state(k):
            copy.start()

    def add(k, way, s, with_ring):
        @pl.loop(0, height(k) // ROWS)
        def _(i):
            r = pl.ds(pl.multiple_of(i * ROWS, ROWS), ROWS)
            total = mine[k][s, way, r, :].astype(jnp.float32) + theirs[k][s, way, r, :].astype(jnp.float32)
            if with_ring:
                total += ring[k][s - 1, way, r, :].astype(jnp.float32)
            mine[k][s, way, r, :] = total.astype(jnp.bfloat16)

    for k, way in pieces:
        load(k, way, 0).wait()
        swap(k, way, 0).wait_recv()
        add(k, way, 0, False)
        hop(k, way, 0).start()

    @pl.loop(1, chips - 1)
    def _(s):
        for k, way in pieces:
            load(k, way, s).wait()
            swap(k, way, s).wait_recv()
            hop(k, way, s - 1).wait_recv()
            add(k, way, s, True)
            hop(k, way, s).start()

    last = chips - 1
    squares[...] = jnp.zeros_like(squares)

    def fold(x):
        return sum(x[:, c : c + LANES] for c in range(0, x.shape[1], LANES))

    for k, way in pieces:
        load(k, way, last).wait()
        swap(k, way, last).wait_recv()
        hop(k, way, last - 1).wait_recv()

        @pl.loop(0, height(k) // ROWS)
        def _(i):
            r = pl.ds(pl.multiple_of(i * ROWS, ROWS), ROWS)
            total = mine[k][last, way, r, :].astype(jnp.float32) + theirs[k][last, way, r, :].astype(jnp.float32)
            total += ring[k][last - 1, way, r, :].astype(jnp.float32)
            g = total.astype(jnp.bfloat16)
            mine[k][last, way, r, :] = g
            g = g.astype(jnp.float32)
            squares[...] += fold(g * g)

    parts[0] = squares[...]
    for d in range(1, n):
        part_to(d).start()
    for k in range(WEIGHTS):
        for copy in state(k):
            copy.wait()
    everything = squares[...]
    for d in range(1, n):
        part_to(d).wait_recv()
        everything = everything + parts[d]
    factor = jnp.minimum(1.0, 0.5 * lax.rsqrt(jnp.full((1, LANES), jnp.sum(everything), jnp.float32) / count + 1e-30))[0, 0]

    for k, way in pieces:
        start = pl.multiple_of(me * height(k), ROWS)

        @pl.loop(0, height(k) // ROWS)
        def _(i):
            r = pl.ds(pl.multiple_of(i * ROWS, ROWS), ROWS)
            at = pl.ds(pl.multiple_of(start + i * ROWS, ROWS), ROWS)
            g = mine[k][last, way, r, :].astype(jnp.float32) * factor
            w = whole[k][way, at, :].astype(jnp.float32)
            new_m = 0.9 * m[k][way, r, :] + 0.1 * g
            new_v = 0.95 * v[k][way, r, :] + 0.05 * g * g
            m[k][way, r, :] = new_m
            v[k][way, r, :] = new_v
            change = new_m * lax.rsqrt(new_v + 1e-8) + 0.1 * w
            whole[k][way, at, :] = (w - 0.02 * change).astype(jnp.bfloat16)

        pass_on(k, way, 0).start()
        give(k, way, 0).start()

    @pl.loop(0, chips - 2)
    def _(s):
        for k, way in pieces:
            arrived(k, way, s).wait_recv()
            pass_on(k, way, s + 1).start()
            give(k, way, s + 1).start()

    for k, way in pieces:
        arrived(k, way, last - 1).wait_recv()
        give(k, way, last).start()

    for d in range(1, n):
        part_to(d).wait_send()

    @pl.loop(0, chips)
    def _(s):
        for k, way in pieces:
            swap(k, way, s).wait_send()
            given(k, way, s).wait_recv()

    @pl.loop(0, chips - 1)
    def _(s):
        for k, way in pieces:
            hop(k, way, s).wait_send()
            pass_on(k, way, s).wait_send()

    @pl.loop(0, chips)
    def _(s):
        for k, way in pieces:
            give(k, way, s).wait_send()


def solution(mesh):
    n = mesh.shape["dp"]
    chips = n // CORES

    def step(*arrays):
        terms, weights, m, v = (arrays[i : i + 3] for i in (0, 3, 6, 9))
        count = float(sum(w.size for w in weights))
        whole = [pltpu.VMEM(w.shape, w.dtype) for w in weights]
        moments = [pltpu.VMEM(a.shape, a.dtype) for a in (*m, *v)]
        blocks = [a.shape for a in m]
        dma = pltpu.SemaphoreType.DMA
        two = (WEIGHTS, 2)
        return pl.pallas_call(
            functools.partial(step_kernel, n, count),
            out_shape=(*whole, *moments),
            in_specs=[pl.BlockSpec(memory_space=pl.ANY)] * 12,
            out_specs=[pl.BlockSpec(memory_space=pltpu.VMEM)] * 9,
            scratch_shapes=[
                *(pltpu.VMEM((chips, *b), jnp.bfloat16) for b in blocks),
                *(pltpu.VMEM((chips, *b), jnp.bfloat16) for b in blocks),
                *(pltpu.VMEM((chips - 1, *b), jnp.bfloat16) for b in blocks),
                pltpu.VMEM((ROWS, LANES), jnp.float32),
                pltpu.VMEM((n, ROWS, LANES), jnp.float32),
                dma((*two, chips)),
                dma((*two, chips)),
                dma((*two, chips)),
                dma((*two, chips - 1)),
                dma((*two, chips - 1)),
                dma((*two, chips - 1)),
                dma((*two, chips - 1)),
                dma((*two, chips)),
                dma((*two, chips)),
                dma((WEIGHTS, 4)),
                dma((n,)),
                dma((n,)),
            ],
            compiler_params=pltpu.CompilerParams(collective_id=0, has_side_effects=True, vmem_limit_bytes=34 * 2**20),
        )(*arrays)

    all_of, cut = P(None, None, None), P(None, "dp", None)
    return jax.shard_map(
        step,
        mesh=mesh,
        in_specs=(P(("rep", "dp"), None, None, None),) * 3 + (all_of,) * 3 + (cut,) * 6,
        out_specs=(P("rep", None, None),) * 3 + (P("rep", "dp", None),) * 6,
        check_vma=False,
    )
```

time: 392 us -> 195 us (0.50)
  waiting for transfers between devices: 266 us -> 0 us
  Pallas kernels: 0 us -> 182 us
  local copies, waits for them, and re-layouts: 71.8 us -> 12.5 us
  blocking collectives: 27.3 us -> 0 us
  between operations: 16.9 us -> 0.66 us
  other arithmetic: 9.36 us -> 0 us
    pallas_call x0 -> x1, Pallas kernels: none -> 182 us  [step(): pl.pallas_call(functools.partial(step_kernel, n, count), out_shape=(*whol...]
    unnamed x9 -> x0, waiting for transfers between devices: 147 us -> none
    all_gather x3 -> x0, waiting for transfers between devices: 119 us -> none  [step(): whole = [lax.all_gather(one[0], 'dp', axis=1, tiled=True) for one in new]]
    unnamed x22 -> x9, local copies, waits for them, and re-layouts: 71.8 us -> 12.5 us
    psum x1 -> x0, blocking collectives: 27.3 us -> none  [step(): squares = lax.psum(sum((jnp.sum(g * g) for g in gradients)), 'dp')]
    convert_element_type x3 -> x0, other arithmetic: 7.78 us -> none  [adamw(): return ((w - 0.02 * step).astype(jnp.bfloat16), m, v)]
  transfers between devices with their start and end apart: 6 -> 0, of which waited for: 6 -> 0; matrix products, arithmetic and copies ran while one was open for 13% -> 0% of each run, Pallas kernels for 0% -> 0%
where the time goes in v1:
time: 195 us
  Pallas kernels  182 us (93%)
  local copies, waits for them, and re-layouts  12.5 us (6%)
    pallas_call x1, Pallas kernels, step(): pl.pallas_call(functools.partial(step_kernel, n, count), out_shape=(*whol...  182 us
    unnamed x9, local copies, waits for them, and re-layouts  12.5 us

profile of v1, /device:TPU:21, one launch (start us, length us, event | category | flops | bytes accessed | tf_op | source)
XLA Modules:
  0.0 195.4 jit_solution(7722354311447295013)
XLA Ops:
  0.6 182.2 %shard_map.187 = (bf16[2,640,2176]{2,1,0:T(8,128)(2,1)S(1)}, bf16[2,640,2176]{2,1,0:T(8,128)(2,1)S(1)}, bf16[2,2176,640]{2,1,0:T(8,128)(2,1)S(1)}, f32[2,40,2176...) custom-call(bf16[1,2,640,2176]{3,2,1,0:T(8,128)(2,1)} %refs_0_.1, ...), custom_call_target="tpu_custom_call" | custom-call | tf_op jit(solution)/shard_map/pallas_call | solution.py:235
  182.9 2.5 %copy.30 = bf16[2,640,2176]{2,1,0:T(8,128)(2,1)} copy(bf16[2,640,2176]{2,1,0:T(8,128)(2,1)S(1)} %get-tuple-element.9) | data formatting | bytes 11141120
  185.3 0.8 copy.33
  186.2 0.8 copy.34
  187.0 0.8 copy.35
  187.9 0.8 copy.36
  188.7 0.8 copy.37
  189.6 0.8 copy.38
  190.4 2.5 %copy.31 = bf16[2,640,2176]{2,1,0:T(8,128)(2,1)} copy(bf16[2,640,2176]{2,1,0:T(8,128)(2,1)S(1)} %get-tuple-element.10) | data formatting | bytes 11141120
  192.9 2.5 %copy.32 = bf16[2,2176,640]{2,1,0:T(8,128)(2,1)} copy(bf16[2,2176,640]{2,1,0:T(8,128)(2,1)S(1)} %get-tuple-element.11) | data formatting | bytes 11141120

commit v2 on v1

--- a/solution.py
+++ b/solution.py
@@ -220,6 +220,20 @@
             give(k, way, s).wait_send()
 
 
+def store_kernel(*refs):
+    half = len(refs) // 2
+    results, outs, sems = refs[:half], refs[half:-1], refs[-1]
+    copies = [
+        pltpu.make_async_copy(a.at[layer], b.at[layer], sems.at[i, layer])
+        for i, (a, b) in enumerate(zip(results, outs, strict=True))
+        for layer in range(a.shape[0])
+    ]
+    for copy in copies:
+        copy.start()
+    for copy in copies:
+        copy.wait()
+
+
 def solution(mesh):
     n = mesh.shape["dp"]
     chips = n // CORES
@@ -232,7 +246,7 @@
         blocks = [a.shape for a in m]
         dma = pltpu.SemaphoreType.DMA
         two = (WEIGHTS, 2)
-        return pl.pallas_call(
+        results = pl.pallas_call(
             functools.partial(step_kernel, n, count),
             out_shape=(*whole, *moments),
             in_specs=[pl.BlockSpec(memory_space=pl.ANY)] * 12,
@@ -258,6 +272,14 @@
             ],
             compiler_params=pltpu.CompilerParams(collective_id=0, has_side_effects=True, vmem_limit_bytes=34 * 2**20),
         )(*arrays)
+        return pl.pallas_call(
+            store_kernel,
+            out_shape=[jax.ShapeDtypeStruct(a.shape, a.dtype) for a in results],
+            in_specs=[pl.BlockSpec(memory_space=pltpu.VMEM)] * 9,
+            out_specs=[pl.BlockSpec(memory_space=pl.ANY)] * 9,
+            scratch_shapes=[dma((9, 2))],
+            compiler_params=pltpu.CompilerParams(vmem_limit_bytes=2**20),
+        )(*results)
 
     all_of, cut = P(None, None, None), P(None, "dp", None)
     return jax.shard_map(

time: 195 us -> 190 us (0.974)
  local copies, waits for them, and re-layouts: 12.5 us -> 0 us
  Pallas kernels: 182 us -> 189 us
    unnamed x9 -> x0, local copies, waits for them, and re-layouts: 12.5 us -> none
    pallas_call x0 -> x1, Pallas kernels: none -> 7.23 us  [step(): pl.pallas_call(store_kernel, out_shape=[jax.ShapeDtypeStruct(a.shape, a.d...]
where the time goes in v2:
time: 190 us
  Pallas kernels  189 us (99%)
    pallas_call x1, Pallas kernels, step(): pl.pallas_call(functools.partial(step_kernel, n, count), out_shape=(*whol...  182 us
    pallas_call x1, Pallas kernels, step(): pl.pallas_call(store_kernel, out_shape=[jax.ShapeDtypeStruct(a.shape, a.d...  7.23 us

profile of v2, /device:TPU:21, one launch (start us, length us, event | category | flops | bytes accessed | tf_op | source)
XLA Modules:
  0.0 190.1 jit_solution(2267891051668940380)
XLA Ops:
  0.6 182.2 %shard_map.187 = (bf16[2,640,2176]{2,1,0:T(8,128)(2,1)S(1)}, bf16[2,640,2176]{2,1,0:T(8,128)(2,1)S(1)}, bf16[2,2176,640]{2,1,0:T(8,128)(2,1)S(1)}, f32[2,40,2176...) custom-call(bf16[1,2,640,2176]{3,2,1,0:T(8,128)(2,1)} %refs_0_.1, ...), custom_call_target="tpu_custom_call" | custom-call | tf_op jit(solution)/shard_map/pallas_call | solution.py:249
  182.9 7.2 %shard_map.188 = (bf16[2,640,2176]{2,1,0:T(8,128)(2,1)}, bf16[2,640,2176]{2,1,0:T(8,128)(2,1)}, bf16[2,2176,640]{2,1,0:T(8,128)(2,1)}, f32[2,40,2176]{2,1,0:T(8,...) custom-call(bf16[2,640,2176]{2,1,0:T(8,128)(2,1)S(1)} %get-tuple-ele, ...), custom_call_target="tpu_custom_call" | custom-call | tf_op jit(solution)/shard_map/pallas_call | solution.py:275

commit v3 on v2

--- a/solution.py
+++ b/solution.py
@@ -24,7 +24,7 @@
     whole, m, v = three(), three(), three()
     mine, theirs, ring = three(), three(), three()
     squares, parts = next(take), next(take)
-    (load_sem, swap_send, swap_recv, ring_send, ring_recv, gather_send, gather_recv, give_send, give_recv, state_sem, part_send, part_recv) = take
+    load_sem, swap_send, swap_recv, ring_send, hop_recv, gather_send, give_send, give_recv, state_sem, part_sem = take
 
     chips = n // CORES
     me = lax.axis_index("dp")
@@ -45,19 +45,22 @@
 
     pieces = [(k, way) for k in range(WEIGHTS) for way in (0, 1)]
 
+    def first(s):
+        return 0 if isinstance(s, int) and s == 0 else 1
+
     def load(k, way, s):
         at = (chip_at(way, s + 1) * CORES + core) * height(k)
-        return pltpu.make_async_copy(rows_of(grads[k], (0, way), at, height(k)), mine[k].at[s, way], load_sem.at[k, way, s])
-
-    def swap(k, way, s):
+        return pltpu.make_async_copy(rows_of(grads[k], (0, way), at, height(k)), mine[k].at[s, way], load_sem.at[k, first(s)])
+
+    def swap(k, way, s, slot):
         at = (chip_at(way, s + 1) * CORES + 1 - core) * height(k)
         return pltpu.make_async_remote_copy(
-            rows_of(grads[k], (0, way), at, height(k)), theirs[k].at[s, way], swap_send.at[k, way, s], swap_recv.at[k, way, s], **to(other)
+            rows_of(grads[k], (0, way), at, height(k)), theirs[k].at[s, way], swap_send.at[k], swap_recv.at[k, slot], **to(other)
         )
 
     def hop(k, way, s):
         return pltpu.make_async_remote_copy(
-            mine[k].at[s, way], ring[k].at[s, way], ring_send.at[k, way, s], ring_recv.at[k, way, s], **to(toward[way])
+            mine[k].at[s, way], ring[k].at[s, way], ring_send.at[k], hop_recv.at[k, way, s], **to(toward[way])
         )
 
     def place(k, way, back, at_core):
@@ -65,34 +68,31 @@
 
     def pass_on(k, way, s):
         block = place(k, way, s, core)
-        return pltpu.make_async_remote_copy(block, block, gather_send.at[k, way, s], gather_recv.at[k, way, s], **to(toward[way]))
+        return pltpu.make_async_remote_copy(block, block, gather_send.at[k], hop_recv.at[k, way, s], **to(toward[way]))
 
     def give(k, way, s):
         block = place(k, way, s, core)
-        return pltpu.make_async_remote_copy(block, block, give_send.at[k, way, s], give_recv.at[k, way, s], **to(other))
-
-    def arrived(k, way, s):
-        block = place(k, way, s + 1, core)
-        return pltpu.make_async_remote_copy(block, block, gather_send.at[k, way, s], gather_recv.at[k, way, s], **to(toward[way]))
-
-    def given(k, way, s):
-        block = place(k, way, s, 1 - core)
-        return pltpu.make_async_remote_copy(block, block, give_send.at[k, way, s], give_recv.at[k, way, s], **to(other))
-
-    def state(k):
+        return pltpu.make_async_remote_copy(block, block, give_send.at[k], give_recv.at[k], **to(other))
+
+    def await_bytes(ref, sem):
+        pltpu.make_async_copy(ref, ref, sem).wait()
+
+    def await_hop(k, way, s):
+        await_bytes(ring[k].at[s, way], hop_recv.at[k, way, s])
+
+    def start_state(k):
         for way in (0, 1):
-            yield pltpu.make_async_copy(
-                rows_of(old[k], (way,), me * height(k), height(k)), place(k, way, 0, core), state_sem.at[k, way]
-            )
-        yield pltpu.make_async_copy(m_in[k], m[k], state_sem.at[k, 2])
-        yield pltpu.make_async_copy(v_in[k], v[k], state_sem.at[k, 3])
+            pltpu.make_async_copy(rows_of(old[k], (way,), me * height(k), height(k)), place(k, way, 0, core), state_sem.at[k, 0]).start()
+        pltpu.make_async_copy(m_in[k], m[k], state_sem.at[k, 1]).start()
+        pltpu.make_async_copy(v_in[k], v[k], state_sem.at[k, 2]).start()
+
+    def await_state(k):
+        await_bytes(mine[k].at[0], state_sem.at[k, 0])
+        await_bytes(m[k], state_sem.at[k, 1])
+        await_bytes(v[k], state_sem.at[k, 2])
 
     def part_to(d):
-        peer = lax.rem(me + d, n)
-        return pltpu.make_async_remote_copy(parts.at[0], parts.at[d], part_send.at[d], part_recv.at[d], **to(peer))
-
-    for k, way in pieces:
-        load(k, way, 0).start()
+        return pltpu.make_async_remote_copy(parts.at[0], parts.at[d], part_sem.at[0], part_sem.at[1], **to(lax.rem(me + d, n)))
 
     barrier = pltpu.get_barrier_semaphore()
     for device in (other, ahead, behind):
@@ -100,17 +100,20 @@
     pl.semaphore_wait(barrier, 3)
 
     for k, way in pieces:
-        swap(k, way, 0).start()
-
-    @pl.loop(1, chips)
+        swap(k, way, 0, way).start()
+        load(k, way, 0).start()
+    for k, way in pieces:
+        swap(k, way, 1, 2).start()
+        load(k, way, 1).start()
+
+    @pl.loop(2, chips)
     def _(s):
         for k, way in pieces:
-            swap(k, way, s).start()
+            swap(k, way, s, 3).start()
             load(k, way, s).start()
 
     for k in range(WEIGHTS):
-        for copy in state(k):
-            copy.start()
+        start_state(k)
 
     def add(k, way, s, with_ring):
         @pl.loop(0, height(k) // ROWS)
@@ -122,20 +125,33 @@
             mine[k][s, way, r, :] = total.astype(jnp.bfloat16)
 
     for k, way in pieces:
-        load(k, way, 0).wait()
-        swap(k, way, 0).wait_recv()
+        if way == 0:
+            await_bytes(mine[k].at[0], load_sem.at[k, 0])
+        await_bytes(theirs[k].at[0, way], swap_recv.at[k, way])
         add(k, way, 0, False)
         hop(k, way, 0).start()
 
-    @pl.loop(1, chips - 1)
+    for k, way in pieces:
+        if way == 0:
+            await_bytes(mine[k].at[pl.ds(1, chips - 1)], load_sem.at[k, 1])
+            await_bytes(theirs[k].at[1], swap_recv.at[k, 2])
+        await_hop(k, way, 0)
+        add(k, way, 1, True)
+        hop(k, way, 1).start()
+
+    for k in range(WEIGHTS):
+        await_bytes(theirs[k].at[pl.ds(2, chips - 2)], swap_recv.at[k, 3])
+
+    @pl.loop(2, chips - 1)
     def _(s):
         for k, way in pieces:
-            load(k, way, s).wait()
-            swap(k, way, s).wait_recv()
-            hop(k, way, s - 1).wait_recv()
+            await_hop(k, way, s - 1)
             add(k, way, s, True)
             hop(k, way, s).start()
 
+    for k in range(WEIGHTS):
+        await_state(k)
+
     last = chips - 1
     squares[...] = jnp.zeros_like(squares)
 
@@ -143,9 +159,7 @@
         return sum(x[:, c : c + LANES] for c in range(0, x.shape[1], LANES))
 
     for k, way in pieces:
-        load(k, way, last).wait()
-        swap(k, way, last).wait_recv()
-        hop(k, way, last - 1).wait_recv()
+        await_hop(k, way, last - 1)
 
         @pl.loop(0, height(k) // ROWS)
         def _(i):
@@ -157,17 +171,12 @@
             g = g.astype(jnp.float32)
             squares[...] += fold(g * g)
 
-    parts[0] = squares[...]
-    for d in range(1, n):
+    parts[0] = jnp.sum(squares[...], axis=0, keepdims=True)
+    for d in sorted(range(1, n), key=lambda d: -min(d, n - d)):
         part_to(d).start()
-    for k in range(WEIGHTS):
-        for copy in state(k):
-            copy.wait()
-    everything = squares[...]
-    for d in range(1, n):
-        part_to(d).wait_recv()
-        everything = everything + parts[d]
-    factor = jnp.minimum(1.0, 0.5 * lax.rsqrt(jnp.full((1, LANES), jnp.sum(everything), jnp.float32) / count + 1e-30))[0, 0]
+    await_bytes(parts.at[pl.ds(1, n - 1)], part_sem.at[1])
+    everything = sum(parts[d] for d in range(n))
+    factor = jnp.minimum(1.0, 0.5 * lax.rsqrt(jnp.sum(everything, keepdims=True) / count + 1e-30))[0, 0]
 
     for k, way in pieces:
         start = pl.multiple_of(me * height(k), ROWS)
@@ -191,33 +200,22 @@
     @pl.loop(0, chips - 2)
     def _(s):
         for k, way in pieces:
-            arrived(k, way, s).wait_recv()
+            await_hop(k, way, s)
             pass_on(k, way, s + 1).start()
             give(k, way, s + 1).start()
 
     for k, way in pieces:
-        arrived(k, way, last - 1).wait_recv()
+        await_hop(k, way, last - 1)
         give(k, way, last).start()
 
-    for d in range(1, n):
-        part_to(d).wait_send()
-
-    @pl.loop(0, chips)
-    def _(s):
-        for k, way in pieces:
-            swap(k, way, s).wait_send()
-            given(k, way, s).wait_recv()
-
-    @pl.loop(0, chips - 1)
-    def _(s):
-        for k, way in pieces:
-            hop(k, way, s).wait_send()
-            pass_on(k, way, s).wait_send()
-
-    @pl.loop(0, chips)
-    def _(s):
-        for k, way in pieces:
-            give(k, way, s).wait_send()
+    await_bytes(parts.at[pl.ds(1, n - 1)], part_sem.at[0])
+    for k in range(WEIGHTS):
+        everywhere = whole[k].at[:, pl.ds(0, chips * height(k))]
+        await_bytes(mine[k], swap_send.at[k])
+        await_bytes(mine[k].at[pl.ds(0, last)], ring_send.at[k])
+        await_bytes(mine[k].at[pl.ds(0, last)], gather_send.at[k])
+        await_bytes(everywhere, give_recv.at[k])
+        await_bytes(everywhere, give_send.at[k])
 
 
 def store_kernel(*refs):
@@ -245,7 +243,6 @@
         moments = [pltpu.VMEM(a.shape, a.dtype) for a in (*m, *v)]
         blocks = [a.shape for a in m]
         dma = pltpu.SemaphoreType.DMA
-        two = (WEIGHTS, 2)
         results = pl.pallas_call(
             functools.partial(step_kernel, n, count),
             out_shape=(*whole, *moments),
@@ -256,19 +253,17 @@
                 *(pltpu.VMEM((chips, *b), jnp.bfloat16) for b in blocks),
                 *(pltpu.VMEM((chips - 1, *b), jnp.bfloat16) for b in blocks),
                 pltpu.VMEM((ROWS, LANES), jnp.float32),
-                pltpu.VMEM((n, ROWS, LANES), jnp.float32),
-                dma((*two, chips)),
-                dma((*two, chips)),
-                dma((*two, chips)),
-                dma((*two, chips - 1)),
-                dma((*two, chips - 1)),
-                dma((*two, chips - 1)),
-                dma((*two, chips - 1)),
-                dma((*two, chips)),
-                dma((*two, chips)),
+                pltpu.VMEM((n, 1, LANES), jnp.float32),
+                dma((WEIGHTS, 2)),
+                dma((WEIGHTS,)),
                 dma((WEIGHTS, 4)),
-                dma((n,)),
-                dma((n,)),
+                dma((WEIGHTS,)),
+                dma((WEIGHTS, 2, chips - 1)),
+                dma((WEIGHTS,)),
+                dma((WEIGHTS,)),
+                dma((WEIGHTS,)),
+                dma((WEIGHTS, 3)),
+                dma((2,)),
             ],
             compiler_params=pltpu.CompilerParams(collective_id=0, has_side_effects=True, vmem_limit_bytes=34 * 2**20),
         )(*arrays)

time: 190 us -> 186 us (0.979)
  Pallas kernels: 189 us -> 185 us
    pallas_call x1, Pallas kernels: 182 us -> 178 us  [step(): pl.pallas_call(functools.partial(step_kernel, n, count), out_shape=(*whol...]
where the time goes in v3:
time: 186 us
  Pallas kernels  185 us (99%)
    pallas_call x1, Pallas kernels, step(): pl.pallas_call(functools.partial(step_kernel, n, count), out_shape=(*whol...  178 us
    pallas_call x1, Pallas kernels, step(): pl.pallas_call(store_kernel, out_shape=[jax.ShapeDtypeStruct(a.shape, a.d...  7.23 us

profile of v3, /device:TPU:21, one launch (start us, length us, event | category | flops | bytes accessed | tf_op | source)
XLA Modules:
  0.0 186.1 jit_solution(12497197591628802236)
XLA Ops:
  0.6 178.2 %shard_map.187 = (bf16[2,640,2176]{2,1,0:T(8,128)(2,1)S(1)}, bf16[2,640,2176]{2,1,0:T(8,128)(2,1)S(1)}, bf16[2,2176,640]{2,1,0:T(8,128)(2,1)S(1)}, f32[2,40,2176...) custom-call(bf16[1,2,640,2176]{3,2,1,0:T(8,128)(2,1)} %refs_0_.1, ...), custom_call_target="tpu_custom_call" | custom-call | tf_op jit(solution)/shard_map/pallas_call | solution.py:246
  178.9 7.2 %shard_map.188 = (bf16[2,640,2176]{2,1,0:T(8,128)(2,1)}, bf16[2,640,2176]{2,1,0:T(8,128)(2,1)}, bf16[2,2176,640]{2,1,0:T(8,128)(2,1)}, f32[2,40,2176]{2,1,0:T(8,...) custom-call(bf16[2,640,2176]{2,1,0:T(8,128)(2,1)S(1)} %get-tuple-ele, ...), custom_call_target="tpu_custom_call" | custom-call | tf_op jit(solution)/shard_map/pallas_call | solution.py:270
